TPU v7x, 256 devices: a whole 4x4x8 slice. The times are simulated.
256 devices in a mesh: batch: 16 (over y, x), field: 2 (over core), dim: 8 (over z).
Axes of the slice: x: 4, y: 4, z: 8, core: 2. Of those that a mesh axis runs over, the one named last changes fastest.
Arguments:
- features: bfloat16 [26, 128, 16384], P('field', 'dim', 'batch'), may hold values from -6 to 6
- cross_weight: bfloat16 [2, 26, 128, 26, 128], P(None, 'field', 'dim'), may hold values from -0.109375 to 0.109375
- cross_bias: float32 [2, 26, 128], P(None, 'field', 'dim'), may hold values from -3 to 3
- tower_weight: bfloat16 [1024, 26, 128], P(('field', 'dim')), may hold values from -0.109375 to 0.109375
- tower_bias: float32 [1024], P(('field', 'dim')), may hold values from -3 to 3
- query_weight: bfloat16 [1024, 128], P(('field', 'dim')), may hold values from -0.1875 to 0.1875
- user_vec: bfloat16 [16384, 128], P('batch'), may hold values from -6 to 6
- candidates: bfloat16 [4096, 128], P('batch'), may hold values from -6 to 6
- positive: int32 [16384], P('batch'), may hold values from 0 to 4095
Outputs:
- crossed: bfloat16 [26, 128, 16384], P('field', 'dim', 'batch')
- losses: float32 [16384], P('batch')
All inputs are finite; a program needn't handle non-finite values.
Results may differ from a plain program's by a relative error of at most 0.0049.
Values may be sent and summed in bfloat16 or wider, within the bound.
A program may use at most 64 MiB of HBM per device.

v0:
```python
import math
import jax
import jax.numpy as jnp
from jax import lax
from jax.sharding import Mesh
from jax.sharding import PartitionSpec as P

CROSS = 2
BATCH = ("batch_0", "batch_1")


def whole_of(x, axes, dim):
    if not axes:
        return x
    nearer = lax.all_gather(x, axes[-1], axis=dim, tiled=True)
    return whole_of(nearer, axes[:-1], dim)


def cut_along(x, dim, length):
    shape = x.shape
    pieces = x.reshape(*shape[:dim], length, shape[dim] // length, *shape[dim + 1 :])
    return jnp.moveaxis(pieces, dim, 0)


def summed_on_arrival(x, axis, dim):
    length = lax.axis_size(axis)
    pieces = lax.all_to_all(cut_along(x, dim, length), axis, 0, 0, tiled=True)
    return jnp.sum(pieces.astype(jnp.float32), axis=0)


def laid_out(pieces, dim):
    shape = list(pieces.shape[1:])
    shape[dim] *= pieces.shape[0]
    return jnp.moveaxis(pieces, 0, dim).reshape(shape)


def sent_to_all(x, axis):
    copies = jnp.broadcast_to(x, (lax.axis_size(axis), *x.shape))
    return lax.all_to_all(copies, axis, split_axis=0, concat_axis=0, tiled=True)


def gather_directly(x, axis, dim):
    return laid_out(sent_to_all(x, axis), dim)


def by_device(weights, field_count, dim_count):
    out_count, fields_all, entries_all = weights.shape
    shaped = weights.reshape(
        out_count, field_count, fields_all // field_count, dim_count, entries_all // dim_count
    )
    shaped = shaped.transpose(1, 3, 0, 2, 4)
    return shaped.reshape(
        field_count * dim_count, out_count, fields_all // field_count * (entries_all // dim_count)
    )


def row_adder(blocks, shards):
    return jnp.einsum("kib,koi->ob", shards, blocks, preferred_element_type=jnp.float32)


def cross_flat(current, blocks):
    field_local, entry_local, row_count = current.shape
    flattened = current.reshape(1, field_local * entry_local, row_count)
    return row_adder(blocks, lax.all_gather(flattened, ("field", "dim"), axis=0, tiled=True))


def next_layer(anchor, current, product, bias_vec):
    field_local, entry_local, row_count = current.shape
    gated = (product + bias_vec.reshape(field_local * entry_local, 1)).reshape(
        field_local, entry_local, row_count
    )
    return (anchor * gated + current.astype(jnp.float32)).astype(jnp.bfloat16)


def candidate_loss(query_vec, targets, candidates):
    score_scale = 1.0 / math.sqrt(query_vec.shape[1])
    row_count = query_vec.shape[0]
    running_max = jnp.full((row_count,), -1e30, jnp.float32)
    logits = (
        jnp.einsum(
            "be,ce->bc",
            query_vec,
            whole_of(candidates, BATCH, 0),
            preferred_element_type=jnp.float32,
        )
        * score_scale
    )
    labels = lax.broadcasted_iota(jnp.int32, logits.shape, 1)
    picked = jnp.sum(jnp.where(labels == targets[:, None], logits, 0.0), axis=1)
    new_max = jnp.maximum(running_max, jnp.max(logits, axis=1))
    running_sum = jnp.sum(jnp.exp(logits - new_max[:, None]), axis=1)
    best_score, exp_total, picked = (new_max, running_sum, picked)
    return best_score + jnp.log(exp_total) - picked


def body(
    features,
    cross_weight,
    cross_bias,
    tower_weight,
    tower_bias,
    query_weight,
    user_vec,
    candidates,
    positive,
):
    field_count = lax.axis_size("field")
    dim_count = lax.axis_size("dim")
    field_local, entry_local, row_count = features.shape
    column_count = field_local * entry_local
    anchor = features.astype(jnp.float32)
    current = features
    stacked = cross_weight.reshape(
        CROSS, column_count, cross_weight.shape[3], cross_weight.shape[4]
    )
    for level_idx in range(CROSS):
        blocks = by_device(stacked[level_idx], field_count, dim_count)
        product = cross_flat(current, blocks)
        current = next_layer(anchor, current, product, cross_bias[level_idx])
    tower_blocks = by_device(tower_weight, field_count, dim_count)
    flattened = current.reshape(1, column_count, row_count)
    tower_pre = row_adder(
        tower_blocks, lax.all_gather(flattened, ("field", "dim"), axis=0, tiled=True)
    )
    hidden = jax.nn.relu(tower_pre + tower_bias[:, None]).astype(jnp.bfloat16)
    partial_value = lax.dot_general(
        hidden, query_weight, (((0,), (0,)), ((), ())), preferred_element_type=jnp.float32
    )
    share_rows = row_count // (field_count * dim_count)
    member = lax.axis_index(("field", "dim"))
    query_part = summed_on_arrival(partial_value.astype(jnp.bfloat16), ("field", "dim"), 0)
    user_rows = lax.dynamic_slice_in_dim(user_vec, member * share_rows, share_rows, 0)
    targets = lax.dynamic_slice_in_dim(positive, member * share_rows, share_rows, 0)
    query_vec = (query_part + user_rows.astype(jnp.float32)).astype(jnp.bfloat16)
    part_loss = candidate_loss(query_vec, targets, candidates)
    losses = gather_directly(part_loss, ("field", "dim"), 0)
    return (current, losses)


def solution(mesh):
    torus = Mesh(
        mesh.devices.reshape(4, 4, mesh.shape["field"], mesh.shape["dim"]),
        ("batch_0", "batch_1", "field", "dim"),
    )
    in_specs = (
        P("field", "dim", BATCH),
        P(None, "field", "dim", None, None),
        P(None, "field", "dim"),
        P(("field", "dim"), None, None),
        P(("field", "dim")),
        P(("field", "dim"), None),
        P(BATCH, None),
        P(BATCH, None),
        P(BATCH),
    )
    out_specs = (P("field", "dim", BATCH), P(BATCH))
    return jax.shard_map(body, mesh=torus, in_specs=in_specs, out_specs=out_specs, check_vma=False)
```

profile of v0, /device:TPU:1, one launch (start us, length us, event | category | flops | bytes accessed | tf_op | source)
XLA Modules:
  0.0 219.8 jit_solution(14988092904554589448)
XLA Ops:
  7.2 0.7 all-gather.5.cloned.1.call-update
  8.0 2.2 %fusion.13 = (bf16[1,13,16,26,128]{4,2,3,1,0:T(8,128)(2,1)S(1)}, bf16[1,13,16,26,128]{4,2,3,1,0:T(8,128)(2,1)S(1)}) fusion(bf16[2,13,16,26,128]{4,2,3,1,0:T(8,128)(2,1)} %param.10), kind=kLoop, calls=%fused_computation.29 | loop fusion | bytes 5537792 | tf_op jit(solution)/shard_map/slice | solution.py:117
  10.2 0.2 copy.19
  10.4 8.7 %reshape_squeeze.8 = bf16[208,2,13,8,16]{4,3,0,2,1:T(8,128)(2,1)} reshape(bf16[1,13,16,26,128]{4,2,1,3,0:T(8,128)(2,1)S(1)} %copy.19) | data formatting | bytes 2768896 | tf_op jit(solution)/shard_map/reshape;squeeze | solution.py:48
  19.1 10.9 %copy.20 = bf16[2,8,208,13,16]{2,4,3,1,0:T(8,128)(2,1)S(1)} copy(bf16[2,8,208,13,16]{4,1,2,3,0:T(8,128)(2,1)} %bitcast.50) | data formatting | bytes 2768896 | tf_op jit(solution)/shard_map/transpose | solution.py:51
  30.1 0.1 add.51
  30.2 32.3 %all-gather.5.cloned.1.call-done = bf16[16,208,1024]{2,1,0:T(8,128)(2,1)} async-done(((bf16[1,208,1024]{2,1,0:T(8,128)(2,1)}), bf16[16,208,1024]{2,1,0:T(8,128)(2,1)}) %all-gather.5.cloned.1.call-update) | async-done | bytes 6815760 | tf_op jit(solution)/shard_map/all_gather | solution.py:64
  62.5 4.6 %fusion = f32[208,1024]{1,0:T(8,128)S(1)} fusion(bf16[16,208,208]{1,2,0:T(8,128)(2,1)S(1)} %bitcast.52, bf16[16,208,1024]{2,1,0:T(8,128)(2,1)} %all-gather.5.cloned.1.call-done, f32[208]{0:T(256)S(1)} %add.51), kind=kOutput, calls=%fused_computation.4 | convolution fusion | flops 1417887744 | bytes 9052992 | tf_op jit(solution)/shard_map/kib,koi->ob/dot_general | solution.py:58
  67.1 0.9 fusion.7
  68.0 0.0 all-gather.9.cloned.1.call-start
  68.1 0.2 copy.22
  68.3 8.7 %reshape_squeeze.9 = bf16[208,2,13,8,16]{4,3,0,2,1:T(8,128)(2,1)} reshape(bf16[1,13,16,26,128]{4,2,1,3,0:T(8,128)(2,1)S(1)} %copy.22) | data formatting | bytes 2768896 | tf_op jit(solution)/shard_map/reshape;squeeze | solution.py:48
  77.0 11.2 %copy.23 = bf16[2,8,208,13,16]{2,4,3,1,0:T(8,128)(2,1)S(1)} copy(bf16[2,8,208,13,16]{4,1,2,3,0:T(8,128)(2,1)} %bitcast.51) | data formatting | bytes 2768896 | tf_op jit(solution)/shard_map/transpose | solution.py:51
  88.2 0.1 add.55
  88.2 26.9 %all-gather.7.cloned.1.call-done = bf16[16,208,1024]{2,1,0:T(8,128)(2,1)} async-done(((bf16[1,208,1024]{2,1,0:T(8,128)(2,1)}), bf16[16,208,1024]{2,1,0:T(8,128)(2,1)}) %all-gather.7.cloned.1.call-update) | async-done | bytes 6815760 | tf_op jit(solution)/shard_map/all_gather | solution.py:64
  115.2 4.6 %fusion.1 = f32[1024,208]{0,1:T(8,128)S(1)} fusion(bf16[16,208,1024]{2,1,0:T(8,128)(2,1)} %all-gather.7.cloned.1.call-done, bf16[16,208,208]{1,2,0:T(8,128)(2,1)S(1)} %bitcast.58, f32[208]{0:T(256)S(1)} %add.55), kind=kOutput, calls=%fused_computation.5 | convolution fusion | flops 1417887744 | bytes 9052992 | tf_op jit(solution)/shard_map/kib,koi->ob/dot_general | solution.py:58
  119.9 1.0 fusion.6
  120.9 10.4 %all_gather.18 = bf16[1024,128]{1,0:T(8,128)(2,1)} all-gather(bf16[256,128]{1,0:T(8,128)(2,1)S(1)} %copy-done.4), channel_id=1, replica_groups=mesh['batch_0'=4,'batch_1'=4,'field'=2,'dim'=8] {'batch_1'}, dimensions={0}, use_global_device_ids=true | all-gather | bytes 327680 | tf_op jit(solution)/shard_map/all_gather | solution.py:15
  131.4 0.4 copy.25
  131.8 0.1 copy.26
  132.0 36.0 %all-gather.9.cloned.1.call-done = bf16[16,208,1024]{2,1,0:T(8,128)(2,1)} async-done(((bf16[1,208,1024]{2,1,0:T(8,128)(2,1)}), bf16[16,208,1024]{2,1,0:T(8,128)(2,1)}) %all-gather.9.cloned.1.call-update) | async-done | bytes 6815760 | tf_op jit(solution)/shard_map/all_gather | solution.py:123
  168.0 5.3 %convolution_convert_fusion = bf16[1024,128]{1,0:T(8,128)(2,1)} fusion(bf16[64,128]{1,0:T(8,128)(2,1)S(1)} %copy-done, bf16[16,208,1024]{2,1,0:T(8,128)(2,1)} %all-gather.9.cloned.1.call-done, bf16[16,64,208]{1,2,0:T(8,128)(2,1)S(1)} %bitcast.56, f32[64]{0:T(128)S(1)} %copy-done.6), kind=kOutput, calls=%fused_computation.6 | convolution fusion | flops 453312512 | bytes 7520512 | tf_op jit(solution)/shard_map/dot_general | solution.py:126
  173.3 4.6 %all-to-all-start = ((bf16[16,64,128]{2,1,0:T(8,128)(2,1)}), bf16[16,64,128]{2,1,0:T(8,128)(2,1)S(1)}, u32[]{:S(2)}, u32[]{:S(2)}) async-start(bf16[16,64,128]{2,1,0:T(8,128)(2,1)} %bitcast.16), calls=%async_computation | async-start | bytes 524288 | tf_op jit(solution)/shard_map/all_to_all | solution.py:27
  177.9 0.8 dynamic_slice.7
  178.6 8.9 %all-to-all-done = bf16[16,64,128]{2,1,0:T(8,128)(2,1)S(1)} async-done(((bf16[16,64,128]{2,1,0:T(8,128)(2,1)}), bf16[16,64,128]{2,1,0:T(8,128)(2,1)S(1)}, u32[]{:S(2)}, u32[]{:S(2)}) %all-to-all-start) | async-done | bytes 262176 | tf_op jit(solution)/shard_map/all_to_all | solution.py:27
  187.5 4.9 %all-gather.11.cloned.1.call-done = bf16[4096,128]{1,0:T(8,128)(2,1)} async-done(((bf16[1024,128]{1,0:T(8,128)(2,1)}), bf16[4096,128]{1,0:T(8,128)(2,1)}) %all-gather.11.cloned.1.call-update) | async-done | bytes 1048592 | tf_op jit(solution)/shard_map/all_gather | solution.py:15
  192.5 1.8 fusion.14
  194.3 0.5 exponential_reduce_fusion
  194.8 16.6 %all_to_all.11 = f32[16,1,64]{2,1,0:T(1,128)S(1)} all-to-all(f32[16,1,64]{2,1,0:T(1,128)S(1)} %broadcast_in_dim.15), channel_id=1, replica_groups=mesh['batch_0'=4,'batch_1'=4,'field'=2,'dim'=8] {'field','dim'}, dimensions={0} | all-to-all | bytes 8192 | tf_op jit(solution)/shard_map/all_to_all | solution.py:39
  211.4 0.5 broadcast.18
  211.9 0.7 reduce.7
  212.6 0.7 reshape.64
  (25 shorter events, 0.3 us)
Async XLA Ops:
  7.2 160.8 %copy-start = (bf16[64,128]{1,0:T(8,128)(2,1)S(1)}, bf16[64,128]{1,0:T(8,128)(2,1)}, u32[]{:S(2)}) copy-start(bf16[64,128]{1,0:T(8,128)(2,1)} %param.14) | copy-start | bytes 49156
  7.2 55.3 %all-gather.5.cloned.1.call-start = ((), (), s32[]{:S(2)}) async-start(), calls=%async_computation.2 | async-start | bytes 7241728 | tf_op jit(solution)/shard_map/all_gather | solution.py:64
  7.9 107.3 %all-gather.7.cloned.1.call-start = ((), (), s32[]{:S(2)}) async-start(), calls=%async_computation.3 | async-start | bytes 7241728 | tf_op jit(solution)/shard_map/all_gather | solution.py:64
  19.1 11.0 %copy-start.5 = (f32[2,13,16]{2,0,1:T(2,128)S(1)}, f32[2,13,16]{2,0,1:T(2,128)}, u32[]{:S(2)}) copy-start(f32[2,13,16]{2,0,1:T(2,128)} %param.11) | copy-start | bytes 4996
  62.5 4.6 %copy-start.1 = (bf16[13,16,1024]{2,1,0:T(8,128)(2,1)S(1)}, bf16[13,16,1024]{2,1,0:T(8,128)(2,1)}, u32[]{:S(2)}) copy-start(bf16[13,16,1024]{2,1,0:T(8,128)(2,1)} %param.9) | copy-start | bytes 1277956
  68.0 100.0 %all-gather.9.cloned.1.call-start = ((), (), s32[]{:S(2)}) async-start(), calls=%async_computation.4 | async-start | bytes 7241728 | tf_op jit(solution)/shard_map/all_gather | solution.py:123
  115.2 4.7 %copy-start.2 = (bf16[13,16,1024]{2,1,0:T(8,128)(2,1)S(1)}, bf16[13,16,1024]{2,1,0:T(8,128)(2,1)}, u32[]{:S(2)}) copy-start(bf16[13,16,1024]{2,1,0:T(8,128)(2,1)} %fusion.7) | copy-start | bytes 1277956
  115.2 5.7 %copy-start.4 = (bf16[256,128]{1,0:T(8,128)(2,1)S(1)}, bf16[256,128]{1,0:T(8,128)(2,1)}, u32[]{:S(2)}) copy-start(bf16[256,128]{1,0:T(8,128)(2,1)} %param.16) | copy-start | bytes 196612
  119.8 11.6 %copy-start.3 = (bf16[64,26,128]{2,0,1:T(8,128)(2,1)S(1)}, bf16[64,26,128]{2,0,1:T(8,128)(2,1)}, u32[]{:S(2)}) copy-start(bf16[64,26,128]{2,0,1:T(8,128)(2,1)} %param.12) | copy-start | bytes 1277956
  119.8 48.2 %copy-start.6 = (f32[64]{0:T(128)S(1)}, f32[64]{0:T(128)}, u32[]{:S(2)}) copy-start(f32[64]{0:T(128)} %param.13) | copy-start | bytes 772
  120.8 71.6 %all-gather.11.cloned.1.call-start = ((), (), s32[]{:S(2)}) async-start(), calls=%async_computation.5 | async-start | bytes 1310720 | tf_op jit(solution)/shard_map/all_gather | solution.py:15
  173.3 14.2 %all-to-all-start = ((bf16[16,64,128]{2,1,0:T(8,128)(2,1)}), bf16[16,64,128]{2,1,0:T(8,128)(2,1)S(1)}, u32[]{:S(2)}, u32[]{:S(2)}) async-start(bf16[16,64,128]{2,1,0:T(8,128)(2,1)} %bitcast.16), calls=%async_computation | async-start | bytes 524288 | tf_op jit(solution)/shard_map/all_to_all | solution.py:27
Sparse Core Ops, SparseCore 0:
  9.8 52.6 all-gather.4
  68.1 46.9 all-gather.6
  121.0 46.9 all-gather.8
  169.7 22.7 all-gather.10
where the time goes:
time: 220 us
  waiting for transfers between devices  110 us (50%)
  local copies, waits for them, and re-layouts  44.9 us (20%)
  blocking collectives  27 us (12%)
  matrix products  16.3 us (7%)
  between operations  13.9 us (6%)
  starting transfers between devices  4.74 us (2%)
  other arithmetic  3.03 us (1%)
    all_gather x2, waiting for transfers between devices, cross_flat(): lax.all_gather(flattened, ('field', 'dim'), axis=0, tiled=True)  59.2 us
    all_gather x1, waiting for transfers between devices, body(): lax.all_gather(flattened, ('field', 'dim'), axis=0, tiled=True)  36 us
    transpose x3, local copies, waits for them, and re-layouts, by_device(): shaped = shaped.transpose(1, 3, 0, 2, 4)  22.3 us
    another operation x2, local copies, waits for them, and re-layouts, by_device(): weights.reshape(out_count, field_count, fields_all // field_count, dim_co...  17.4 us
    all_to_all x1, blocking collectives, sent_to_all(): return lax.all_to_all(copies, axis, split_axis=0, concat_axis=0, tiled=True)  16.6 us
    all_gather x1, blocking collectives, whole_of(): nearer = lax.all_gather(x, axes[-1], axis=dim, tiled=True)  10.4 us
    dot_general x2, matrix products, row_adder(): jnp.einsum('kib,koi->ob', shards, blocks, preferred_element_type=jnp.floa...  9.24 us
    all_to_all x1, waiting for transfers between devices, summed_on_arrival(): pieces = lax.all_to_all(cut_along(x, dim, length), axis, 0, 0, tiled=True)  8.89 us
  transfers between devices with their start and end apart: 5, of which 5 were waited for; matrix products, arithmetic and copies ran while one was open for 22% of the time, Pallas kernels for 0%

commit v1 on v0

--- a/solution.py
+++ b/solution.py
@@ -7,6 +7,19 @@
 
 CROSS = 2
 BATCH = ("batch_0", "batch_1")
+
+
+def read_chains(inp):
+    new = jnp.concatenate(
+        lax.all_to_all(
+            jnp.stack(lax.axis_size(("field", "dim")) * [inp], axis=0),
+            ("field", "dim"),
+            split_axis=0,
+            concat_axis=0,
+        ),
+        axis=0,
+    )
+    return new
 
 
 def whole_of(x, axes, dim):
@@ -119,9 +132,7 @@
         current = next_layer(anchor, current, product, cross_bias[level_idx])
     tower_blocks = by_device(tower_weight, field_count, dim_count)
     flattened = current.reshape(1, column_count, row_count)
-    tower_pre = row_adder(
-        tower_blocks, lax.all_gather(flattened, ("field", "dim"), axis=0, tiled=True)
-    )
+    tower_pre = row_adder(tower_blocks, read_chains(flattened))
     hidden = jax.nn.relu(tower_pre + tower_bias[:, None]).astype(jnp.bfloat16)
     partial_value = lax.dot_general(
         hidden, query_weight, (((0,), (0,)), ((), ())), preferred_element_type=jnp.float32

time: 220 us -> 324 us (1.47)
  waiting for transfers between devices: 110 us -> 206 us
  starting transfers between devices: 4.74 us -> 11.7 us
  blocking collectives: 27 us -> 22.9 us
  local copies, waits for them, and re-layouts: 44.9 us -> 48.7 us
    all_to_all x0 -> x1, waiting for transfers between devices: none -> 137 us  [read_chains(): lax.all_to_all(jnp.stack(lax.axis_size(('field', 'dim')) * [inp], axis=0)...]
    all_gather x1 -> x0, waiting for transfers between devices: 36 us -> none  [body(): lax.all_gather(flattened, ('field', 'dim'), axis=0, tiled=True)]
    all_gather x1, waiting for transfers between devices: 4.93 us -> 0.03 us  [whole_of(): nearer = lax.all_gather(x, axes[-1], axis=dim, tiled=True)]
    all_to_all x0 -> x1, starting transfers between devices: none -> 4.87 us  [read_chains(): lax.all_to_all(jnp.stack(lax.axis_size(('field', 'dim')) * [inp], axis=0)...]
    all_to_all x1, blocking collectives: 16.6 us -> 11.7 us  [sent_to_all(): return lax.all_to_all(copies, axis, split_axis=0, concat_axis=0, tiled=True)]
    another operation x0 -> x1, local copies, waits for them, and re-layouts: none -> 3.72 us  [read_chains(): jnp.stack(lax.axis_size(('field', 'dim')) * [inp], axis=0)]
  transfers between devices with their start and end apart: 5 -> 5, of which waited for: 5 -> 4; matrix products, arithmetic and copies ran while one was open for 22% -> 15% of each run, Pallas kernels for 0% -> 0%
where the time goes in v1:
time: 324 us; the launch traced here: 323 us
  waiting for transfers between devices  206 us (64%)
  local copies, waits for them, and re-layouts  48.7 us (15%)
  blocking collectives  22.9 us (7%)
  matrix products  16.3 us (5%)
  between operations  15.7 us (5%)
  starting transfers between devices  11.7 us (4%)
    all_to_all x1, waiting for transfers between devices, read_chains(): lax.all_to_all(jnp.stack(lax.axis_size(('field', 'dim')) * [inp], axis=0)...  137 us
    all_gather x2, waiting for transfers between devices, cross_flat(): lax.all_gather(flattened, ('field', 'dim'), axis=0, tiled=True)  59.2 us
    transpose x3, local copies, waits for them, and re-layouts, by_device(): shaped = shaped.transpose(1, 3, 0, 2, 4)  22.3 us
    another operation x2, local copies, waits for them, and re-layouts, by_device(): weights.reshape(out_count, field_count, fields_all // field_count, dim_co...  17.4 us
    all_to_all x1, blocking collectives, sent_to_all(): return lax.all_to_all(copies, axis, split_axis=0, concat_axis=0, tiled=True)  11.7 us
    all_gather x1, blocking collectives, whole_of(): nearer = lax.all_gather(x, axes[-1], axis=dim, tiled=True)  11.1 us
    dot_general x2, matrix products, row_adder(): jnp.einsum('kib,koi->ob', shards, blocks, preferred_element_type=jnp.floa...  9.19 us
    all_to_all x1, waiting for transfers between devices, summed_on_arrival(): pieces = lax.all_to_all(cut_along(x, dim, length), axis, 0, 0, tiled=True)  8.89 us
  transfers between devices with their start and end apart: 5, of which 4 were waited for; matrix products, arithmetic and copies ran while one was open for 15% of the time, Pallas kernels for 0%

profile of v1, /device:TPU:1, one launch (start us, length us, event | category | flops | bytes accessed | tf_op | source)
XLA Modules:
  0.0 323.0 jit_solution(301139899295517346)
XLA Ops:
  8.1 0.7 all-gather.4.cloned.1.call-update
  8.8 2.2 fusion.26
  11.0 0.2 copy.28
  11.3 8.7 %reshape_squeeze.8 = bf16[208,2,13,8,16]{4,3,0,2,1:T(8,128)(2,1)} reshape(bf16[1,13,16,26,128]{4,2,1,3,0:T(8,128)(2,1)S(1)} %copy.28) | data formatting | bytes 2768896 | tf_op jit(solution)/shard_map/reshape;squeeze | solution.py:61
  20.0 10.9 %copy.29 = bf16[2,8,208,13,16]{2,4,3,1,0:T(8,128)(2,1)S(1)} copy(bf16[2,8,208,13,16]{4,1,2,3,0:T(8,128)(2,1)} %bitcast.62) | data formatting | bytes 2768896 | tf_op jit(solution)/shard_map/transpose | solution.py:64
  31.0 0.1 add.51
  31.1 32.3 %all-gather.4.cloned.1.call-done = bf16[16,208,1024]{2,1,0:T(8,128)(2,1)} async-done(((bf16[1,208,1024]{2,1,0:T(8,128)(2,1)}), bf16[16,208,1024]{2,1,0:T(8,128)(2,1)}) %all-gather.4.cloned.1.call-update) | async-done | bytes 6815760 | tf_op jit(solution)/shard_map/all_gather | solution.py:77
  63.3 4.6 %fusion.2 = f32[208,1024]{1,0:T(8,128)S(1)} fusion(bf16[16,208,208]{1,2,0:T(8,128)(2,1)S(1)} %bitcast.64, bf16[16,208,1024]{2,1,0:T(8,128)(2,1)} %all-gather.4.cloned.1.call-done, f32[208]{0:T(256)S(1)} %add.51), kind=kOutput, calls=%fused_computation.6 | convolution fusion | flops 1417887744 | bytes 9052992 | tf_op jit(solution)/shard_map/kib,koi->ob/dot_general | solution.py:71
  68.0 0.9 fusion.20
  68.9 0.2 copy.31
  69.1 8.7 %reshape_squeeze.9 = bf16[208,2,13,8,16]{4,3,0,2,1:T(8,128)(2,1)} reshape(bf16[1,13,16,26,128]{4,2,1,3,0:T(8,128)(2,1)S(1)} %copy.31) | data formatting | bytes 2768896 | tf_op jit(solution)/shard_map/reshape;squeeze | solution.py:61
  77.8 11.2 %copy.32 = bf16[2,8,208,13,16]{2,4,3,1,0:T(8,128)(2,1)S(1)} copy(bf16[2,8,208,13,16]{4,1,2,3,0:T(8,128)(2,1)} %bitcast.63) | data formatting | bytes 2768896 | tf_op jit(solution)/shard_map/transpose | solution.py:64
  89.0 0.1 add.55
  89.0 27.0 %all-gather.6.cloned.1.call-done = bf16[16,208,1024]{2,1,0:T(8,128)(2,1)} async-done(((bf16[1,208,1024]{2,1,0:T(8,128)(2,1)}), bf16[16,208,1024]{2,1,0:T(8,128)(2,1)}) %all-gather.6.cloned.1.call-update) | async-done | bytes 6815760 | tf_op jit(solution)/shard_map/all_gather | solution.py:77
  116.0 4.6 %fusion.3 = f32[1024,208]{0,1:T(8,128)S(1)} fusion(bf16[16,208,1024]{2,1,0:T(8,128)(2,1)} %all-gather.6.cloned.1.call-done, bf16[16,208,208]{1,2,0:T(8,128)(2,1)S(1)} %bitcast.71, f32[208]{0:T(256)S(1)} %add.55), kind=kOutput, calls=%fused_computation.7 | convolution fusion | flops 1417887744 | bytes 9052992 | tf_op jit(solution)/shard_map/kib,koi->ob/dot_general | solution.py:71
  120.6 0.2 fusion.19
  120.8 3.7 %stack.3 = bf16[16,1,208,1024]{3,2,1,0:T(8,128)(2,1)} broadcast(bf16[208,1024]{1,0:T(8,128)(2,1)S(1)} %bitcast.70), dimensions={2,3} | broadcast | bytes 7241728 | tf_op jit(solution)/shard_map/stack | solution.py:15
  124.5 4.9 %all-to-all-start = ((bf16[16,1,208,1024]{3,2,1,0:T(8,128)(2,1)}), bf16[16,1,208,1024]{3,2,1,0:T(8,128)(2,1)}, u32[]{:S(2)}, u32[]{:S(2)}) async-start(bf16[16,1,208,1024]{3,2,1,0:T(8,128)(2,1)} %stack.3), calls=%async_computation | async-start | bytes 13631488 | tf_op jit(solution)/shard_map/all_to_all | solution.py:14
  129.5 11.1 %all_gather.14 = bf16[1024,128]{1,0:T(8,128)(2,1)} all-gather(bf16[256,128]{1,0:T(8,128)(2,1)S(1)} %copy-done.5), channel_id=1, replica_groups=mesh['batch_0'=4,'batch_1'=4,'field'=2,'dim'=8] {'batch_1'}, dimensions={0}, use_global_device_ids=true | all-gather | bytes 327680 | tf_op jit(solution)/shard_map/all_gather | solution.py:28
  140.6 0.4 copy.34
  141.1 0.1 copy.35
  141.2 136.8 %all-to-all-done = bf16[16,1,208,1024]{3,2,1,0:T(8,128)(2,1)} async-done(((bf16[16,1,208,1024]{3,2,1,0:T(8,128)(2,1)}), bf16[16,1,208,1024]{3,2,1,0:T(8,128)(2,1)}, u32[]{:S(2)}, u32[]{:S(2)}) %all-to-all-start) | async-done | bytes 6815776 | tf_op jit(solution)/shard_map/all_to_all | solution.py:14
  278.0 5.2 %convolution_convert_fusion = bf16[1024,128]{1,0:T(8,128)(2,1)} fusion(bf16[64,128]{1,0:T(8,128)(2,1)S(1)} %copy-done, bf16[16,64,208]{1,2,0:T(8,128)(2,1)S(1)} %bitcast.68, bf16[16,1,208,1024]{3,2,1,0:T(8,128)(2,1)} %all-to-all-done, f32[64]{0:T(128)S(1)} %copy-done.7), kind=kOutput, calls=%fused_computation.8 | convolution fusion | flops 453312512 | bytes 7520512 | tf_op jit(solution)/shard_map/dot_general | solution.py:137
  283.2 6.7 %all-to-all-start.1 = ((bf16[16,64,128]{2,1,0:T(8,128)(2,1)}), bf16[16,64,128]{2,1,0:T(8,128)(2,1)S(1)}, u32[]{:S(2)}, u32[]{:S(2)}) async-start(bf16[16,64,128]{2,1,0:T(8,128)(2,1)} %bitcast.17), calls=%async_computation.1 | async-start | bytes 524288 | tf_op jit(solution)/shard_map/all_to_all | solution.py:40
  290.0 0.8 dynamic_slice.7
  290.7 8.9 %all-to-all-done.1 = bf16[16,64,128]{2,1,0:T(8,128)(2,1)S(1)} async-done(((bf16[16,64,128]{2,1,0:T(8,128)(2,1)}), bf16[16,64,128]{2,1,0:T(8,128)(2,1)S(1)}, u32[]{:S(2)}, u32[]{:S(2)}) %all-to-all-start.1) | async-done | bytes 262176 | tf_op jit(solution)/shard_map/all_to_all | solution.py:40
  299.7 1.8 fusion.27
  301.5 0.5 exponential_reduce_fusion
  302.0 11.7 %all_to_all.16 = f32[16,1,64]{2,1,0:T(1,128)S(1)} all-to-all(f32[16,1,64]{2,1,0:T(1,128)S(1)} %broadcast_in_dim.15), channel_id=1, replica_groups=mesh['batch_0'=4,'batch_1'=4,'field'=2,'dim'=8] {'field','dim'}, dimensions={0} | all-to-all | bytes 8192 | tf_op jit(solution)/shard_map/all_to_all | solution.py:52
  313.7 0.5 broadcast.20
  314.3 0.7 reduce.7
  314.9 0.7 reshape.68
  (27 shorter events, 0.3 us)
Async XLA Ops:
  8.0 270.0 %copy-start = (bf16[64,128]{1,0:T(8,128)(2,1)S(1)}, bf16[64,128]{1,0:T(8,128)(2,1)}, u32[]{:S(2)}) copy-start(bf16[64,128]{1,0:T(8,128)(2,1)} %param.14) | copy-start | bytes 49156
  8.0 55.3 %all-gather.4.cloned.1.call-start = ((), (), s32[]{:S(2)}) async-start(), calls=%async_computation.3 | async-start | bytes 7241728 | tf_op jit(solution)/shard_map/all_gather | solution.py:77
  8.7 107.3 %all-gather.6.cloned.1.call-start = ((), (), s32[]{:S(2)}) async-start(), calls=%async_computation.4 | async-start | bytes 7241728 | tf_op jit(solution)/shard_map/all_gather | solution.py:77
  20.0 11.0 %copy-start.6 = (f32[2,13,16]{2,0,1:T(2,128)S(1)}, f32[2,13,16]{2,0,1:T(2,128)}, u32[]{:S(2)}) copy-start(f32[2,13,16]{2,0,1:T(2,128)} %param.11) | copy-start | bytes 4996
  63.3 4.6 %copy-start.1 = (bf16[13,16,1024]{2,1,0:T(8,128)(2,1)S(1)}, bf16[13,16,1024]{2,1,0:T(8,128)(2,1)}, u32[]{:S(2)}) copy-start(bf16[13,16,1024]{2,1,0:T(8,128)(2,1)} %param.9) | copy-start | bytes 1277956
  89.0 31.6 %copy-start.2 = (bf16[13,16,1024]{2,1,0:T(8,128)(2,1)S(1)}, bf16[13,16,1024]{2,1,0:T(8,128)(2,1)}, u32[]{:S(2)}) copy-start(bf16[13,16,1024]{2,1,0:T(8,128)(2,1)} %fusion.20) | copy-start | bytes 1277956
  120.8 3.7 %copy-start.3 = (bf16[13,16,1024]{2,1,0:T(8,128)(2,1)}, bf16[13,16,1024]{2,1,0:T(8,128)(2,1)S(1)}, u32[]{:S(2)}) copy-start(bf16[13,16,1024]{2,1,0:T(8,128)(2,1)S(1)} %fusion.19) | copy-start | bytes 1277956
  124.5 4.9 %copy-start.5 = (bf16[256,128]{1,0:T(8,128)(2,1)S(1)}, bf16[256,128]{1,0:T(8,128)(2,1)}, u32[]{:S(2)}) copy-start(bf16[256,128]{1,0:T(8,128)(2,1)} %param.16) | copy-start | bytes 196612
  124.5 16.1 %copy-start.4 = (bf16[64,26,128]{2,0,1:T(8,128)(2,1)S(1)}, bf16[64,26,128]{2,0,1:T(8,128)(2,1)}, u32[]{:S(2)}) copy-start(bf16[64,26,128]{2,0,1:T(8,128)(2,1)} %param.12) | copy-start | bytes 1277956
  124.5 153.5 %copy-start.7 = (f32[64]{0:T(128)S(1)}, f32[64]{0:T(128)}, u32[]{:S(2)}) copy-start(f32[64]{0:T(128)} %param.13) | copy-start | bytes 772
  124.5 153.5 %all-to-all-start = ((bf16[16,1,208,1024]{3,2,1,0:T(8,128)(2,1)}), bf16[16,1,208,1024]{3,2,1,0:T(8,128)(2,1)}, u32[]{:S(2)}, u32[]{:S(2)}) async-start(bf16[16,1,208,1024]{3,2,1,0:T(8,128)(2,1)} %stack.3), calls=%async_computation | async-start | bytes 13631488 | tf_op jit(solution)/shard_map/all_to_all | solution.py:14
  129.4 170.3 %all-gather.8.cloned.1.call-start = ((), (), s32[]{:S(2)}) async-start(), calls=%async_computation.5 | async-start | bytes 1310720 | tf_op jit(solution)/shard_map/all_gather | solution.py:28
  283.2 16.4 %all-to-all-start.1 = ((bf16[16,64,128]{2,1,0:T(8,128)(2,1)}), bf16[16,64,128]{2,1,0:T(8,128)(2,1)S(1)}, u32[]{:S(2)}, u32[]{:S(2)}) async-start(bf16[16,64,128]{2,1,0:T(8,128)(2,1)} %bitcast.17), calls=%async_computation.1 | async-start | bytes 524288 | tf_op jit(solution)/shard_map/all_to_all | solution.py:40
Sparse Core Ops, SparseCore 0:
  10.6 52.6 all-gather.3
  69.0 46.9 all-gather.5
Sparse Core Ops, SparseCore 1:
  140.7 27.1 all-gather.7
